TPU v7x, 32 devices: a whole 2x2x4 slice. The times are simulated.
32 devices in a mesh: grp: 2 (over y), tok: 4 (over z), feat: 4 (over x, core).
Axes of the slice: x: 2, y: 2, z: 4, core: 2. Of those that a mesh axis runs over, the one named last changes fastest.
Arguments:
- acts: bfloat16 [6144, 28672], P(('grp', 'tok'), 'feat'), parts along dimension 0, may hold values from -6 to 6
- grads: bfloat16 [6144, 8192], P(('grp', 'tok'), 'feat'), parts along dimension 0, may hold values from -6 to 6
- proj_in: bfloat16 [28672, 512], P('feat'), may hold values from -0.03125 to 0.03125
- proj_out: bfloat16 [8192, 512], P('feat'), may hold values from -0.0625 to 0.0625
- doc_lengths: int32 [8], P('grp'), parts along dimension 0, may hold values from 1 to 1536, 3072 in all
- doc_owner: int32 [8], P('grp'), parts along dimension 0, may hold values from 0 to 3, as said below
Outputs:
- doc_grads: float32 [8, 512, 512], P(('grp', 'tok'), 'feat'), parts along dimension 0
There are 2 independent parts, one for each index of `grp`. A program takes and returns all parts, laid end to end along the dimension named above; an argument that names none is the same for every part. Nothing has to cross between parts.
Inputs may be any that keep to these rules, and one draw needn't show every extreme that they name: `doc_lengths`: the lengths sum to 3072; the largest is exactly 1536. `doc_owner`: every index along tok owns exactly 1 documents.
All inputs are finite; a program needn't handle non-finite values.
Results may differ from a plain program's by a relative error of at most 0.0043.
Values may be sent and summed in bfloat16 or wider, within the bound.
No kernel may reach another device: no remote copies, remote signals or barrier semaphores. Data moves between devices by JAX's collectives and lax.ppermute only.
A program may use at most 64 MiB of HBM per device.

v0:
```python
import jax
import jax.numpy as jnp
from jax import lax
from jax.sharding import PartitionSpec as P


def outer_sum(weight_cols, low_out, low_in):
    width = weight_cols.shape[1]
    row_share = low_out.shape[1]
    weighted = (low_out[:, None, :] * weight_cols[:, :, None]).reshape(
        low_out.shape[0], width * row_share
    )
    product = lax.dot_general(
        weighted, low_in, (((0,), (0,)), ((), ())), preferred_element_type=jnp.float32
    )
    return product.reshape(width, row_share, low_in.shape[1])


def shards(acts, grads, proj_in, proj_out, doc_lengths, doc_owner):
    tok_rows = acts.shape[0]
    doc_count = doc_lengths.shape[0]
    slot_count = doc_count // lax.axis_size("tok")
    part_in = jnp.dot(acts, proj_in, preferred_element_type=jnp.float32)
    part_out = jnp.dot(grads, proj_out, preferred_element_type=jnp.float32)
    full_in = lax.psum(part_in, "feat")
    grad_part = lax.psum_scatter(part_out, "feat", scatter_dimension=1, tiled=True)
    in_low = full_in.astype(jnp.bfloat16)
    out_low = grad_part.astype(jnp.bfloat16)
    doc_ends = jnp.cumsum(doc_lengths)
    doc_starts = doc_ends - doc_lengths
    doc_index = jnp.arange(doc_count, dtype=jnp.int32)
    same_owner = doc_owner[:, None] == doc_owner[None, :]
    earlier = doc_index[:, None] < doc_index[None, :]
    slot_rank = jnp.sum((same_owner & earlier).astype(jnp.int32), axis=0)
    target = doc_owner * slot_count + slot_rank
    matches = target[:, None] == doc_index[None, :]
    routing = matches.astype(jnp.bfloat16)
    own_first = lax.axis_index("tok") * slot_count
    position = lax.axis_index("tok") * tok_rows + jnp.arange(tok_rows, dtype=jnp.int32)
    member = (
        (position[:, None] >= doc_starts[None, :]) & (position[:, None] < doc_ends[None, :])
    ).astype(jnp.bfloat16)
    all_weights = jnp.dot(member, routing, preferred_element_type=jnp.float32).astype(jnp.bfloat16)
    totals = lax.psum_scatter(
        outer_sum(all_weights, out_low, in_low), "tok", scatter_dimension=0, tiled=True
    )
    slot_lengths = jnp.sum(jnp.where(matches, doc_lengths[:, None], 0), axis=0)
    own_lengths = lax.dynamic_slice_in_dim(slot_lengths, own_first, slot_count, 0)
    scaling = lax.rsqrt(own_lengths.astype(jnp.float32))
    return totals * scaling[:, None, None]


def solution(mesh):
    in_specs = (
        P(("grp", "tok"), "feat"),
        P(("grp", "tok"), "feat"),
        P("feat", None),
        P("feat", None),
        P("grp"),
        P("grp"),
    )
    out_specs = P(("grp", "tok"), "feat", None)
    return jax.shard_map(shards, mesh=mesh, in_specs=in_specs, out_specs=out_specs, check_vma=False)
```

profile of v0, /device:TPU:0, one launch (start us, length us, event | category | flops | bytes accessed | tf_op | source)
XLA Modules:
  0.0 109.7 jit_solution(2129140301364226923)
XLA Ops:
  6.5 0.0 copy-start
  6.5 0.0 copy-start.1
  6.5 0.0 reduce-scatter.3.cloned.1.call-start
  6.5 1.9 %copy-done = bf16[768,2048]{1,0:T(8,128)(2,1)S(1)} copy-done((bf16[768,2048]{1,0:T(8,128)(2,1)S(1)}, bf16[768,2048]{1,0:T(8,128)(2,1)}, u32[]{:S(2)}) %copy-start) | copy-done | bytes 3145752
  8.4 4.5 %fusion.15 = f32[768,512]{1,0:T(8,128)} fusion(bf16[768,2048]{1,0:T(8,128)(2,1)S(1)} %copy-done, bf16[2048,512]{1,0:T(8,128)(2,1)} %param.9), kind=kOutput, calls=%fused_computation.23 | convolution fusion | flops 1610612736 | bytes 6815744 | tf_op jit(solution)/shard_map/dot_general | solution.py:24
  13.0 0.0 reduce-scatter.3.cloned.1.call-update
  13.0 0.0 reduce-scatter.5.cloned.1.call-start
  13.0 0.0 copy-done.1
  13.1 0.1 convert_reduce_fusion
  13.1 0.0 copy-start.2
  13.1 11.6 %fusion.16 = f32[768,512]{1,0:T(8,128)} fusion(bf16[768,7168]{1,0:T(8,128)(2,1)} %param.6, bf16[7168,512]{1,0:T(8,128)(2,1)} %param.8), kind=kOutput, calls=%fused_computation.24 | convolution fusion | flops 5637144576 | bytes 19922944 | tf_op jit(solution)/shard_map/dot_general | solution.py:23
  24.8 0.0 copy-done.2
  24.8 0.2 reduce-window.8
  25.0 0.3 convolution_convert_fusion
  25.2 43.7 %all-reduce.1 = bf16[768,512]{1,0:T(8,128)(2,1)} all-reduce(f32[768,512]{1,0:T(8,128)} %fusion.16), channel_id=1, replica_groups=mesh['grp'=2,'tok'=4,'feat'=4] {'feat'}, use_global_device_ids=true, to_apply=%region_3.4 | all-reduce | flops 393216 | bytes 2359296 | tf_op jit(solution)/shard_map/psum | solution.py:25
  68.9 0.0 reduce-scatter.3.cloned.1.call-done
  68.9 1.0 convert_element_type.17
  70.0 0.1 copy.9
  70.1 2.7 %fusion = f32[4,128,512]{2,1,0:T(8,128)} fusion(bf16[768,512]{1,0:T(8,128)(2,1)} %all-reduce.1, bf16[768,4]{0,1:T(4,128)(2,1)S(1)} %convolution_convert_fusion, bf16[768,128]{0,1:T(8,128)(2,1)S(1)} %copy.9), kind=kOutput, calls=%fused_computation.1 | convolution fusion | flops 403046400 | bytes 2037760 | tf_op jit(solution)/shard_map/dot_general | solution.py:13
  72.8 0.0 reduce-scatter.5.cloned.1.call-update
  72.8 0.1 select_reduce_fusion
  72.9 0.6 dynamic_slice.3
  74.2 26.9 %reduce-scatter.5.cloned.1.call-done = f32[1,128,512]{2,1,0:T(8,128)} async-done(((f32[4,128,512]{2,1,0:T(8,128)}), f32[1,128,512]{2,1,0:T(8,128)}) %reduce-scatter.5.cloned.1.call-update) | async-done | bytes 262160 | tf_op jit(solution)/shard_map/reduce_scatter | solution.py:44
  101.1 1.7 %broadcast_multiply_fusion = f32[1,128,512]{2,1,0:T(8,128)} fusion(f32[1,128,512]{2,1,0:T(8,128)} %reduce-scatter.5.cloned.1.call-done, f32[]{:T(128)} %bitcast.6), kind=kLoop, calls=%fused_computation.8 | loop fusion | flops 65536 | bytes 524292 | tf_op jit(solution)/shard_map/mul | solution.py:50
  (3 shorter events, 0.0 us)
Async XLA Ops:
  6.5 1.9 %copy-start = (bf16[768,2048]{1,0:T(8,128)(2,1)S(1)}, bf16[768,2048]{1,0:T(8,128)(2,1)}, u32[]{:S(2)}) copy-start(bf16[768,2048]{1,0:T(8,128)(2,1)} %param.7) | copy-start | bytes 9437188
  6.5 6.5 %copy-start.1 = (s32[4]{0:T(128)S(1)}, s32[4]{0:T(128)}, u32[]{:S(2)}) copy-start(s32[4]{0:T(128)} %param.11) | copy-start | bytes 52
  6.5 62.4 %reduce-scatter.3.cloned.1.call-start = ((), (), s32[]{:S(2)}) async-start(), calls=%async_computation.2 | async-start | bytes 1966080 | tf_op jit(solution)/shard_map/reduce_scatter | solution.py:26
  13.0 88.2 %reduce-scatter.5.cloned.1.call-start = ((), (), s32[]{:S(2)}) async-start(), calls=%async_computation.3 | async-start | bytes 1310720 | tf_op jit(solution)/shard_map/reduce_scatter | solution.py:44
  13.1 11.6 %copy-start.2 = (s32[4]{0:T(128)S(1)}, s32[4]{0:T(128)}, u32[]{:S(2)}) copy-start(s32[4]{0:T(128)} %param.10) | copy-start | bytes 52
Sparse Core Ops, SparseCore 0:
  13.1 39.2 reduce-scatter.2
  73.0 28.1 reduce-scatter.4
where the time goes:
time: 110 us
  blocking collectives  43.7 us (40%)
  waiting for transfers between devices  27 us (25%)
  matrix products  19.1 us (17%)
  between operations  14.1 us (13%)
  other arithmetic  3.05 us (3%)
  local copies, waits for them, and re-layouts  2.62 us (2%)
    psum x1, blocking collectives, shards(): full_in = lax.psum(part_in, 'feat')  43.7 us
    reduce_scatter x1, waiting for transfers between devices, shards(): lax.psum_scatter(outer_sum(all_weights, out_low, in_low), 'tok', scatter_...  26.9 us
    dot_general x1, matrix products, shards(): part_in = jnp.dot(acts, proj_in, preferred_element_type=jnp.float32)  11.6 us
    dot_general x1, matrix products, shards(): part_out = jnp.dot(grads, proj_out, preferred_element_type=jnp.float32)  4.54 us
    dot_general x1, matrix products, outer_sum(): lax.dot_general(weighted, low_in, (((0,), (0,)), ((), ())), preferred_ele...  2.7 us
  transfers between devices with their start and end apart: 2, of which 1 were waited for; matrix products, arithmetic and copies ran while one was open for 12% of the time, Pallas kernels for 0%

commit v1 on v0

--- a/solution.py
+++ b/solution.py
@@ -22,7 +22,7 @@
     slot_count = doc_count // lax.axis_size("tok")
     part_in = jnp.dot(acts, proj_in, preferred_element_type=jnp.float32)
     part_out = jnp.dot(grads, proj_out, preferred_element_type=jnp.float32)
-    full_in = lax.psum(part_in, "feat")
+    full_in = jnp.sum(lax.all_gather(part_in, "feat"), axis=0)
     grad_part = lax.psum_scatter(part_out, "feat", scatter_dimension=1, tiled=True)
     in_low = full_in.astype(jnp.bfloat16)
     out_low = grad_part.astype(jnp.bfloat16)

time: 110 us -> 135 us (1.23)
  waiting for transfers between devices: 27 us -> 91.5 us
  blocking collectives: 43.7 us -> 0 us
  other arithmetic: 3.05 us -> 7.72 us
    all_gather x0 -> x1, waiting for transfers between devices: none -> 46.8 us  [shards(): full_in = jnp.sum(lax.all_gather(part_in, 'feat'), axis=0)]
    psum x1 -> x0, blocking collectives: 43.7 us -> none  [shards(): full_in = lax.psum(part_in, 'feat')]
    reduce_scatter x1, waiting for transfers between devices: 0.01 us -> 18.6 us  [shards(): lax.psum_scatter(part_out, 'feat', scatter_dimension=1, tiled=True)]
    reduce_sum x0 -> x1, other arithmetic: none -> 4.67 us  [shards(): full_in = jnp.sum(lax.all_gather(part_in, 'feat'), axis=0)]
  transfers between devices with their start and end apart: 2 -> 3, of which waited for: 1 -> 3; matrix products, arithmetic and copies ran while one was open for 12% -> 10% of each run, Pallas kernels for 0% -> 0%
where the time goes in v1:
time: 135 us
  waiting for transfers between devices  91.5 us (68%)
  matrix products  19.2 us (14%)
  between operations  13.8 us (10%)
  other arithmetic  7.72 us (6%)
  local copies, waits for them, and re-layouts  2.63 us (2%)
    all_gather x1, waiting for transfers between devices, shards(): full_in = jnp.sum(lax.all_gather(part_in, 'feat'), axis=0)  46.8 us
    reduce_scatter x1, waiting for transfers between devices, shards(): lax.psum_scatter(outer_sum(all_weights, out_low, in_low), 'tok', scatter_...  26.1 us
    reduce_scatter x1, waiting for transfers between devices, shards(): lax.psum_scatter(part_out, 'feat', scatter_dimension=1, tiled=True)  18.6 us
    dot_general x1, matrix products, shards(): part_in = jnp.dot(acts, proj_in, preferred_element_type=jnp.float32)  11.6 us
    reduce_sum x1, other arithmetic, shards(): full_in = jnp.sum(lax.all_gather(part_in, 'feat'), axis=0)  4.67 us
    dot_general x1, matrix products, shards(): part_out = jnp.dot(grads, proj_out, preferred_element_type=jnp.float32)  4.61 us
  transfers between devices with their start and end apart: 3, of which 3 were waited for; matrix products, arithmetic and copies ran while one was open for 10% of the time, Pallas kernels for 0%

profile of v1, /device:TPU:0, one launch (start us, length us, event | category | flops | bytes accessed | tf_op | source)
XLA Modules:
  0.0 134.9 jit_solution(17112977618396546785)
XLA Ops:
  6.5 1.9 %copy-done = bf16[768,2048]{1,0:T(8,128)(2,1)S(1)} copy-done((bf16[768,2048]{1,0:T(8,128)(2,1)S(1)}, bf16[768,2048]{1,0:T(8,128)(2,1)}, u32[]{:S(2)}) %copy-start) | copy-done | bytes 3145752
  8.4 4.6 %fusion.15 = f32[768,512]{1,0:T(8,128)} fusion(bf16[768,2048]{1,0:T(8,128)(2,1)S(1)} %copy-done, bf16[2048,512]{1,0:T(8,128)(2,1)} %param.9), kind=kOutput, calls=%fused_computation.23 | convolution fusion | flops 1610612736 | bytes 6815744 | tf_op jit(solution)/shard_map/dot_general | solution.py:24
  13.0 0.0 reduce-scatter.3.cloned.1.call-update
  13.1 0.0 copy-start.1
  13.1 0.0 copy-start.2
  13.1 0.0 all-gather.3.cloned.1.call-start
  13.1 11.6 %fusion.16 = f32[768,512]{1,0:T(8,128)} fusion(bf16[768,7168]{1,0:T(8,128)(2,1)} %param.6, bf16[7168,512]{1,0:T(8,128)(2,1)} %param.8), kind=kOutput, calls=%fused_computation.24 | convolution fusion | flops 5637144576 | bytes 19922944 | tf_op jit(solution)/shard_map/dot_general | solution.py:23
  24.8 0.0 all-gather.3.cloned.1.call-update
  24.8 0.0 reduce-scatter.5.cloned.1.call-start
  24.9 0.1 convert_reduce_fusion
  25.0 0.0 copy-done.2
  25.0 0.2 reduce-window.8
  25.1 0.3 convolution_convert_fusion
  25.4 18.6 %reduce-scatter.3.cloned.1.call-done = f32[768,128]{1,0:T(8,128)} async-done(((f32[768,512]{1,0:T(8,128)}), f32[768,128]{1,0:T(8,128)}) %reduce-scatter.3.cloned.1.call-update) | async-done | bytes 393232 | tf_op jit(solution)/shard_map/reduce_scatter | solution.py:26
  44.0 1.0 convert_element_type.17
  45.0 0.1 copy.9
  45.1 46.8 %all-gather.3.cloned.1.call-done = f32[3072,512]{1,0:T(8,128)} async-done(((f32[768,512]{1,0:T(8,128)}), f32[3072,512]{1,0:T(8,128)}) %all-gather.3.cloned.1.call-update) | async-done | bytes 6291472 | tf_op jit(solution)/shard_map/all_gather | solution.py:25
  91.9 4.7 %reduce_sum.28 = bf16[768,512]{1,0:T(8,128)(2,1)} reduce(f32[4,768,512]{2,1,0:T(8,128)} %bitcast.19, f32[]{:T(128)} %constant.14.clone.1), dimensions={0}, to_apply=%region_3.4 | reduce | flops 1179648 | bytes 7077892 | tf_op jit(solution)/shard_map/reduce_sum | solution.py:25
  96.6 2.7 %fusion = f32[4,128,512]{2,1,0:T(8,128)} fusion(bf16[768,512]{1,0:T(8,128)(2,1)} %reduce_sum.28, bf16[768,4]{0,1:T(4,128)(2,1)S(1)} %convolution_convert_fusion, bf16[768,128]{0,1:T(8,128)(2,1)S(1)} %copy.9), kind=kOutput, calls=%fused_computation.1 | convolution fusion | flops 403046400 | bytes 2037760 | tf_op jit(solution)/shard_map/dot_general | solution.py:13
  99.3 0.0 reduce-scatter.5.cloned.1.call-update
  99.3 0.1 select_reduce_fusion
  99.4 0.6 dynamic_slice.3
  100.7 26.1 %reduce-scatter.5.cloned.1.call-done = f32[1,128,512]{2,1,0:T(8,128)} async-done(((f32[4,128,512]{2,1,0:T(8,128)}), f32[1,128,512]{2,1,0:T(8,128)}) %reduce-scatter.5.cloned.1.call-update) | async-done | bytes 262160 | tf_op jit(solution)/shard_map/reduce_scatter | solution.py:44
  126.7 1.7 %broadcast_multiply_fusion = f32[1,128,512]{2,1,0:T(8,128)} fusion(f32[1,128,512]{2,1,0:T(8,128)} %reduce-scatter.5.cloned.1.call-done, f32[]{:T(128)} %bitcast.7), kind=kLoop, calls=%fused_computation.8 | loop fusion | flops 65536 | bytes 524292 | tf_op jit(solution)/shard_map/mul | solution.py:50
  (6 shorter events, 0.0 us)
Async XLA Ops:
  6.5 1.9 %copy-start = (bf16[768,2048]{1,0:T(8,128)(2,1)S(1)}, bf16[768,2048]{1,0:T(8,128)(2,1)}, u32[]{:S(2)}) copy-start(bf16[768,2048]{1,0:T(8,128)(2,1)} %param.7) | copy-start | bytes 9437188
  6.5 37.4 %reduce-scatter.3.cloned.1.call-start = ((), (), s32[]{:S(2)}) async-start(), calls=%async_computation.2 | async-start | bytes 1966080 | tf_op jit(solution)/shard_map/reduce_scatter | solution.py:26
  13.1 11.8 %copy-start.1 = (s32[4]{0:T(128)S(1)}, s32[4]{0:T(128)}, u32[]{:S(2)}) copy-start(s32[4]{0:T(128)} %param.11) | copy-start | bytes 52
  13.1 11.9 %copy-start.2 = (s32[4]{0:T(128)S(1)}, s32[4]{0:T(128)}, u32[]{:S(2)}) copy-start(s32[4]{0:T(128)} %param.10) | copy-start | bytes 52
  13.1 78.8 %all-gather.3.cloned.1.call-start = ((), (), s32[]{:S(2)}) async-start(), calls=%async_computation.4 | async-start | bytes 7864320 | tf_op jit(solution)/shard_map/all_gather | solution.py:25
  24.8 101.9 %reduce-scatter.5.cloned.1.call-start = ((), (), s32[]{:S(2)}) async-start(), calls=%async_computation.3 | async-start | bytes 1310720 | tf_op jit(solution)/shard_map/reduce_scatter | solution.py:44
Sparse Core Ops, SparseCore 0:
  13.2 30.7 reduce-scatter.2
  45.5 46.3 all-gather.2
  99.4 27.2 reduce-scatter.4
